TPU v7x, 8 devices: a whole 2x2x1 slice. The times are simulated.
8 devices in a mesh: data: 8 (over z, y, x, core).
Axes of the slice: x: 2, y: 2, z: 1, core: 2. Of those that a mesh axis runs over, the one named last changes fastest.
Arguments:
- tokens: bfloat16 [16384, 512], P('data')
- d_logits: bfloat16 [16384, 32000], P('data')
- w_up: bfloat16 [2, 512, 1376], replicated
- w_down: bfloat16 [2, 1376, 512], replicated
- w_out: bfloat16 [512, 32000], replicated
- proj_up: bfloat16 [2, 512, 128], replicated
- proj_down: bfloat16 [2, 512, 128], replicated
- mom_up: float32 [2, 128, 1376], P(None, None, 'data')
- var_up: float32 [2, 128, 1376], P(None, None, 'data')
- mom_down: float32 [2, 1376, 128], P(None, 'data')
- var_down: float32 [2, 1376, 128], P(None, 'data')
- mom_out: float32 [512, 32000], P(None, 'data')
- var_out: float32 [512, 32000], P(None, 'data')
Outputs:
- output 1: bfloat16 [2, 512, 1376], replicated
- output 2: bfloat16 [2, 1376, 512], replicated
- output 3: bfloat16 [512, 32000], replicated
- output 4: float32 [2, 128, 1376], P(None, None, 'data')
- output 5: float32 [2, 128, 1376], P(None, None, 'data')
- output 6: float32 [2, 1376, 128], P(None, 'data')
- output 7: float32 [2, 1376, 128], P(None, 'data')
- output 8: float32 [512, 32000], P(None, 'data')
- output 9: float32 [512, 32000], P(None, 'data')
All inputs are finite; a program needn't handle non-finite values.
Results may differ from a plain program's by a relative error of at most 0.00413151.
Values are sent between devices in bfloat16 or wider.
A program may use at most 1 GiB of HBM per device.

v0:
```python
import jax
import jax.numpy as jnp
from jax import lax
from jax.sharding import PartitionSpec as P

BETA1 = 0.9
BETA2 = 0.999
EPS = 1e-8
STEP = 4
LR = 0.02
ALPHA = 0.5
LR_HEAD = 0.01
DATA_AXIS = 'data'


def gelu_tanh(values):
    return jax.nn.gelu(values, approximate=True)


def adam_update(gradient, moment_one, moment_two):
    moment_one = BETA1 * moment_one + (1.0 - BETA1) * gradient
    moment_two = BETA2 * moment_two + (1.0 - BETA2) * gradient * gradient
    direction = (moment_one / (1.0 - BETA1 ** STEP)) / (jnp.sqrt(moment_two / (1.0 - BETA2 ** STEP)) + EPS)
    return moment_one, moment_two, direction


def forward_backward(tokens, d_logits, w_up, w_down, w_out):
    num_layers = w_up.shape[0]
    hidden = tokens
    saved_acts = []
    for layer_idx in range(num_layers):
        pre_act = jnp.dot(hidden, w_up[layer_idx], preferred_element_type=jnp.float32).astype(jnp.bfloat16)
        post_act = gelu_tanh(pre_act.astype(jnp.float32)).astype(jnp.bfloat16)
        saved_acts.append((hidden, pre_act, post_act))
        hidden = (hidden.astype(jnp.float32) + jnp.dot(post_act, w_down[layer_idx], preferred_element_type=jnp.float32)).astype(jnp.bfloat16)
    grad_head = jnp.einsum('td,tv->dv', hidden, d_logits, preferred_element_type=jnp.float32)
    grad_hidden = jnp.einsum('tv,dv->td', d_logits, w_out, preferred_element_type=jnp.float32).astype(jnp.bfloat16)
    grads_up = [None] * num_layers
    grads_down = [None] * num_layers
    for layer_idx in reversed(range(num_layers)):
        hidden_in, pre_act, post_act = saved_acts[layer_idx]
        grads_down[layer_idx] = jnp.einsum('tf,td->fd', post_act, grad_hidden, preferred_element_type=jnp.float32)
        d_post = jnp.einsum('td,fd->tf', grad_hidden, w_down[layer_idx], preferred_element_type=jnp.float32)
        gelu_pull = jax.vjp(gelu_tanh, pre_act.astype(jnp.float32))[1]
        d_pre = gelu_pull(d_post)[0].astype(jnp.bfloat16)
        grads_up[layer_idx] = jnp.einsum('td,tf->df', hidden_in, d_pre, preferred_element_type=jnp.float32)
        if layer_idx > 0:
            grad_hidden = (grad_hidden.astype(jnp.float32) + jnp.einsum('tf,df->td', d_pre, w_up[layer_idx], preferred_element_type=jnp.float32)).astype(jnp.bfloat16)
    return grad_head, grads_up, grads_down


def local_step(tokens, d_logits, w_up, w_down, w_out, proj_up, proj_down, mom_up, var_up, mom_down, var_down, mom_out, var_out):
    grad_head, grads_up, grads_down = forward_backward(tokens, d_logits, w_up, w_down, w_out)
    up_weights = []
    down_weights = []
    up_first = []
    up_second = []
    down_first = []
    down_second = []
    for layer_idx in range(len(grads_up)):
        low_up = jnp.einsum('dr,df->rf', proj_up[layer_idx].astype(jnp.float32), grads_up[layer_idx], preferred_element_type=jnp.float32)
        low_down = jnp.einsum('fd,dr->fr', grads_down[layer_idx], proj_down[layer_idx].astype(jnp.float32), preferred_element_type=jnp.float32)
        low_up = lax.psum_scatter(low_up, DATA_AXIS, scatter_dimension=1, tiled=True)
        low_down = lax.psum_scatter(low_down, DATA_AXIS, scatter_dimension=0, tiled=True)
        m_up, v_up, dir_up = adam_update(low_up, mom_up[layer_idx], var_up[layer_idx])
        m_down, v_down, dir_down = adam_update(low_down, mom_down[layer_idx], var_down[layer_idx])
        dir_up = lax.all_gather(dir_up.astype(jnp.bfloat16), DATA_AXIS, axis=1, tiled=True)
        dir_down = lax.all_gather(dir_down.astype(jnp.bfloat16), DATA_AXIS, axis=0, tiled=True)
        step_up = jnp.dot(proj_up[layer_idx], dir_up, preferred_element_type=jnp.float32)
        step_down = jnp.einsum('fr,dr->fd', dir_down, proj_down[layer_idx], preferred_element_type=jnp.float32)
        up_weights.append((w_up[layer_idx].astype(jnp.float32) - LR * ALPHA * step_up).astype(jnp.bfloat16))
        down_weights.append((w_down[layer_idx].astype(jnp.float32) - LR * ALPHA * step_down).astype(jnp.bfloat16))
        up_first.append(m_up)
        up_second.append(v_up)
        down_first.append(m_down)
        down_second.append(v_down)
    head_part = lax.psum_scatter(grad_head, DATA_AXIS, scatter_dimension=1, tiled=True)
    m_out, v_out, dir_out = adam_update(head_part, mom_out, var_out)
    shard_cols = mom_out.shape[1]
    w_out_part = lax.dynamic_slice_in_dim(w_out, lax.axis_index(DATA_AXIS) * shard_cols, shard_cols, axis=1)
    w_out_part = (w_out_part.astype(jnp.float32) - LR_HEAD * dir_out).astype(jnp.bfloat16)
    w_out_new = lax.all_gather(w_out_part, DATA_AXIS, axis=1, tiled=True)
    return (jnp.stack(up_weights), jnp.stack(down_weights), w_out_new,
            jnp.stack(up_first), jnp.stack(up_second), jnp.stack(down_first), jnp.stack(down_second),
            m_out, v_out)


def solution(mesh):
    row_spec = P(DATA_AXIS, None)
    whole = P()
    up_spec = P(None, None, DATA_AXIS)
    down_spec = P(None, DATA_AXIS, None)
    head_spec = P(None, DATA_AXIS)
    in_specs = (row_spec, row_spec, whole, whole, whole, whole, whole, up_spec, up_spec, down_spec, down_spec, head_spec, head_spec)
    out_specs = (whole, whole, whole, up_spec, up_spec, down_spec, down_spec, head_spec, head_spec)
    return jax.shard_map(local_step, mesh=mesh, in_specs=in_specs, out_specs=out_specs, check_vma=False)
```

profile of v0, /device:TPU:0, one launch (start us, length us, event | category | flops | bytes accessed | tf_op | source)
XLA Modules:
  0.0 872.3 jit_solution(17215698555872901079)
XLA Ops:
  7.2 5.3 convolution_convert_fusion.1
  12.5 5.5 add_convert_fusion.2
  18.1 3.4 convolution_convert_fusion
  21.4 2.5 copy-done.10
  23.9 6.4 add_convert_fusion
  30.3 79.5 %fusion.131 = f32[512,32000]{0,1:T(8,128)} fusion(bf16[2048,512]{1,0:T(8,128)(2,1)} %add_convert_fusion, bf16[2048,32000]{1,0:T(8,128)(2,1)} %param.14), kind=kOutput, calls=%fused_computation.163 | convolution fusion | flops 67108864000 | bytes 198705152 | tf_op jit(solution)/shard_map/td,tv->dv/dot_general | solution.py:36
  109.9 0.0 all-gather.6.cloned.1.call-start
  109.9 6.9 constant_dynamic-slice_fusion
  116.9 6.9 copy.72
  123.7 357.1 %reduce-scatter.10.cloned.1.call-done = f32[512,4000]{0,1:T(8,128)} async-done(((f32[512,32000]{0,1:T(8,128)}), f32[512,4000]{0,1:T(8,128)}) %reduce-scatter.10.cloned.1.call-update) | async-done | bytes 8192016 | tf_op jit(solution)/shard_map/reduce_scatter | solution.py:77
  480.8 18.8 %subtract_convert_fusion = (bf16[512,4000]{0,1:T(8,128)(2,1)}, f32[512,4000]{0,1:T(8,128)}, f32[512,4000]{0,1:T(8,128)}) fusion(bf16[512,4000]{0,1:T(8,128)(2,1)} %copy.72, f32[512,4000]{0,1:T(8,128)} %reduce-scatter.10.cloned.1.call-done, f32[512,4000]{0,1:T(8,128)} %param.24, f32[512,4000]{0,1:T(8,128)} %param.25), kind=kLoop, calls=%fused_computation.33 | loop fusion | flops 30720000 | bytes 49152000 | tf_op jit(solution)/shard_map/convert_element_type | solution.py:81
  499.7 78.5 %convolution_convert_fusion.2 = bf16[2048,512]{1,0:T(8,128)(2,1)} fusion(bf16[2048,32000]{1,0:T(8,128)(2,1)} %param.14, bf16[512,32000]{1,0:T(8,128)(2,1)} %param.17), kind=kOutput, calls=%fused_computation.60 | convolution fusion | flops 67109912576 | bytes 165937152 | tf_op jit(solution)/shard_map/tv,dv->td/dot_general | solution.py:37
  578.2 7.8 fusion.48
  586.0 25.5 %fusion.3 = f32[176,128]{1,0:T(8,128)} fusion(f32[1376,128]{1,0:T(8,128)S(1)} %fusion.48), kind=kCustom, calls=%all-reduce-scatter.3 | all-reduce-scatter fusion | flops 180225 | bytes 794624
  611.5 0.7 slice.78
  612.2 1.9 collective-permute-start.3
  614.1 12.7 %fusion.8 = bf16[2048,1376]{0,1:T(8,128)(2,1)} fusion(bf16[2048,1376]{0,1:T(8,128)(2,1)} %copy-done.10, bf16[2048,512]{1,0:T(8,128)(2,1)} %convolution_convert_fusion.2, bf16[2,1376,512]{2,1,0:T(8,128)(2,1)S(1)} %copy-done.1), kind=kOutput, calls=%fused_computation.15 | convolution fusion | flops 2944860160 | bytes 14778368 | tf_op jit(solution)/shard_map/td,fd->tf/dot_general | solution.py:43
  626.7 6.8 convolution_bitcast_fusion
  633.6 25.7 %fusion.1 = f32[128,176]{0,1:T(8,128)} fusion(f32[128,1376]{0,1:T(8,128)S(1)} %convolution_bitcast_fusion), kind=kCustom, calls=%all-reduce-scatter.1 | all-reduce-scatter fusion | flops 180225 | bytes 794624
  659.2 1.3 slice.76
  660.5 2.1 collective-permute-start.1
  662.6 8.4 add_convert_fusion.1
  671.0 15.6 %fusion.24 = bf16[1376,512]{1,0:T(8,128)(2,1)} fusion(bf16[2048,512]{1,0:T(8,128)(2,1)} %param.13, bf16[2048,1376]{0,1:T(8,128)(2,1)} %copy-done.9, bf16[2048,512]{1,0:T(8,128)(2,1)} %add_convert_fusion.1, bf16[2,1376,512]{2,1,0:T(8,128)(2,1)S(1)} %copy-done.1), kind=kOutput, calls=%fused_computation.31 | convolution fusion | flops 5830541312 | bytes 12648448 | tf_op jit(solution)/shard_map/td,tf->df/dot_general | solution.py:46
  686.7 1.9 convolution_bitcast_fusion.1
  688.6 18.3 %fusion = f32[128,176]{0,1:T(8,128)} fusion(f32[128,1376]{0,1:T(8,128)S(1)} %convolution_bitcast_fusion.1), kind=kCustom, calls=%all-reduce-scatter | all-reduce-scatter fusion | flops 180225 | bytes 794624
  706.9 1.3 slice.75
  708.2 1.9 collective-permute-start
  710.1 7.5 fusion.51
  717.6 18.9 %fusion.2 = f32[176,128]{1,0:T(8,128)} fusion(f32[1376,128]{1,0:T(8,128)S(1)} %fusion.51), kind=kCustom, calls=%all-reduce-scatter.2 | all-reduce-scatter fusion | flops 180225 | bytes 794624
  736.5 0.7 slice.77
  737.2 1.9 collective-permute-start.2
  739.1 1.8 fusion.130
  740.9 1.8 fusion.129
  742.7 1.8 fusion.128
  744.5 1.8 fusion.127
  746.3 1.7 concatenate.3
  747.9 1.7 concatenate.1
  749.6 1.7 concatenate
  751.3 0.7 fusion.110
  752.0 13.4 %all-gather.3 = bf16[8,172,128]{2,1,0:T(8,128)(2,1)S(1)} all-gather(bf16[1,172,128]{2,1,0:T(8,128)(2,1)S(1)} %get-tuple-element.43), channel_id=1, replica_groups=mesh['data'=8] {'data'}, dimensions={0}, use_global_device_ids=true | all-gather | bytes 396288 | tf_op jit(solution)/shard_map/all_gather | solution.py:68
  765.4 1.0 fusion.112
  766.4 1.6 fusion.113
  768.0 0.8 pad_maximum_fusion.2
  768.8 11.9 %all-gather.1 = bf16[8,172,128]{2,1,0:T(8,128)(2,1)S(1)} all-gather(bf16[1,172,128]{2,1,0:T(8,128)(2,1)S(1)} %get-tuple-element.49), channel_id=1, replica_groups=mesh['data'=8] {'data'}, dimensions={0}, use_global_device_ids=true | all-gather | bytes 396288 | tf_op jit(solution)/shard_map/all_gather | solution.py:67
  780.7 0.8 reshape.41
  781.5 0.8 reshape.37
  782.3 1.7 copy.60
  783.9 1.7 concatenate.2
  785.6 1.0 fusion.111
  786.6 1.0 pad_maximum_fusion.4
  787.6 0.8 copy.62
  788.4 0.8 copy.63
  789.1 1.7 copy.61
  790.8 11.9 %all-gather.2 = bf16[8,172,128]{2,1,0:T(8,128)(2,1)S(1)} all-gather(bf16[1,172,128]{2,1,0:T(8,128)(2,1)S(1)} %get-tuple-element.40), channel_id=1, replica_groups=mesh['data'=8] {'data'}, dimensions={0}, use_global_device_ids=true | all-gather | bytes 396288 | tf_op jit(solution)/shard_map/all_gather | solution.py:68
  802.7 0.8 reshape.39
  803.4 12.0 %all-gather = bf16[8,172,128]{2,1,0:T(8,128)(2,1)S(1)} all-gather(bf16[1,172,128]{2,1,0:T(8,128)(2,1)} %get-tuple-element.46), channel_id=1, replica_groups=mesh['data'=8] {'data'}, dimensions={0}, use_global_device_ids=true | all-gather | bytes 396288 | tf_op jit(solution)/shard_map/all_gather | solution.py:67
  815.4 0.8 reshape.35
  816.2 1.7 fusion.43
  817.9 2.1 fusion.44
  820.0 0.5 fusion.42
  820.6 0.5 fusion.45
  821.1 1.8 pad_maximum_fusion.1
  822.9 1.8 pad_maximum_fusion
  824.7 40.3 %copy.59 = bf16[512,32000]{1,0:T(8,128)(2,1)} copy(bf16[512,32000]{0,1:T(8,128)(2,1)} %all-gather.6.cloned.1.call-done) | data formatting | bytes 65536000
  (31 shorter events, 0.1 us)
Async XLA Ops:
  7.2 5.3 copy-start
  7.2 473.7 %reduce-scatter.10.cloned.1.call-start = ((), (), s32[]{:S(2)}) async-start(), calls=%async_computation.1 | async-start | bytes 73728000 | tf_op jit(solution)/shard_map/reduce_scatter | solution.py:77
  7.2 5.3 copy-start.8
  12.5 5.5 copy-start.9
  12.5 5.5 copy-start.2
  18.0 3.4 copy-start.11
  21.4 2.5 copy-start.10
  109.9 714.8 %all-gather.6.cloned.1.call-start = ((), (), s32[]{:S(2)}) async-start(), calls=%async_computation.2 | async-start | bytes 36864000 | tf_op jit(solution)/shard_map/all_gather | solution.py:82
  578.2 35.9 %copy-start.1 = (bf16[2,1376,512]{2,1,0:T(8,128)(2,1)S(1)}, bf16[2,1376,512]{2,1,0:T(8,128)(2,1)}, u32[]{:S(2)}) copy-start(bf16[2,1376,512]{2,1,0:T(8,128)(2,1)} %param.16) | copy-start | bytes 8454148
  612.2 134.0 %collective-permute-start.3 = (f32[28,128]{1,0:T(8,128)S(1)}, f32[28,128]{1,0:T(8,128)}, u32[]{:S(2)}, u32[]{:S(2)}) collective-permute-start(f32[28,128]{1,0:T(8,128)S(1)} %slice.78), channel_id=1, source_target_pairs={{0,1},{1,2},{2,3},{3,4},{4,5},{5,6},{6,7}} | collective-permute-start | bytes 43016
  660.5 87.4 %collective-permute-start.1 = (f32[128,28]{0,1:T(8,128)}, f32[128,28]{0,1:T(8,128)}, u32[]{:S(2)}, u32[]{:S(2)}) collective-permute-start(f32[128,28]{0,1:T(8,128)} %slice.76), channel_id=1, source_target_pairs={{0,1},{1,2},{2,3},{3,4},{4,5},{5,6},{6,7}} | collective-permute-start | bytes 43016
  708.2 41.4 %collective-permute-start = (f32[128,28]{0,1:T(8,128)}, f32[128,28]{0,1:T(8,128)}, u32[]{:S(2)}, u32[]{:S(2)}) collective-permute-start(f32[128,28]{0,1:T(8,128)} %slice.75), channel_id=1, source_target_pairs={{0,1},{1,2},{2,3},{3,4},{4,5},{5,6},{6,7}} | collective-permute-start | bytes 43016
  737.2 46.7 %collective-permute-start.2 = (f32[28,128]{1,0:T(8,128)S(1)}, f32[28,128]{1,0:T(8,128)}, u32[]{:S(2)}, u32[]{:S(2)}) collective-permute-start(f32[28,128]{1,0:T(8,128)S(1)} %slice.77), channel_id=1, source_target_pairs={{0,1},{1,2},{2,3},{3,4},{4,5},{5,6},{6,7}} | collective-permute-start | bytes 43016
  803.4 17.1 %copy-start.4 = (bf16[1376,128]{1,0:T(8,128)(2,1)S(1)}, bf16[1376,128]{1,0:T(8,128)(2,1)}, u32[]{:S(2)}) copy-start(bf16[1376,128]{1,0:T(8,128)(2,1)} %reshape.37) | copy-start | bytes 1056772
  816.2 3.8 copy-start.5
  816.2 3.8 copy-start.7
  816.2 4.3 copy-start.3
  816.2 4.4 copy-start.6
Sparse Core Ops, SparseCore 0:
  110.0 370.7 reduce-scatter.9
  499.8 164.1 all-gather.5
where the time goes:
time: 882 us; the launch traced here: 872 us
  waiting for transfers between devices  357 us (40%)
  matrix products  244 us (28%)
  blocking collectives  137 us (16%)
  local copies, waits for them, and re-layouts  82.6 us (9%)
  other arithmetic  28.5 us (3%)
  between operations  14.8 us (2%)
    reduce_scatter x1, waiting for transfers between devices, local_step(): lax.psum_scatter(grad_head, DATA_AXIS, scatter_dimension=1, tiled=True)  357 us
    unnamed x4, blocking collectives  88.4 us
    dot_general x1, matrix products, forward_backward(): jnp.einsum('td,tv->dv', hidden, d_logits, preferred_element_type=jnp.floa...  79.5 us
    dot_general x1, matrix products, forward_backward(): jnp.einsum('tv,dv->td', d_logits, w_out, preferred_element_type=jnp.float32)  78.5 us
    unnamed x42, local copies, waits for them, and re-layouts  68.5 us
    all_gather x2, blocking collectives, local_step(): lax.all_gather(dir_down.astype(jnp.bfloat16), DATA_AXIS, axis=0, tiled=True)  25.2 us
    all_gather x2, blocking collectives, local_step(): lax.all_gather(dir_up.astype(jnp.bfloat16), DATA_AXIS, axis=1, tiled=True)  23.8 us
    convert_element_type x1, other arithmetic, local_step(): (w_out_part.astype(jnp.float32) - LR_HEAD * dir_out).astype(jnp.bfloat16)  18.8 us
  transfers between devices with their start and end apart: 6, of which 1 were waited for; matrix products, arithmetic and copies ran while one was open for 32% of the time, Pallas kernels for 0%

commit v1 on v0

v1 whole, which is shorter than its diff:
```python
import functools

import jax
import jax.numpy as jnp
from jax import lax
from jax.experimental import pallas as pl
from jax.experimental.pallas import tpu as pltpu
from jax.sharding import PartitionSpec as P

BETA1 = 0.9
BETA2 = 0.999
EPS = 1e-8
STEP = 4
LR = 0.02
ALPHA = 0.5
LR_HEAD = 0.01
DATA_AXIS = 'data'
MESH = pl.DeviceIdType.MESH

BLK = 512
SUBS = 8
SHARD = 4000
RING = 6
DRING = 4

GROUP_DEST = (0, 1, 0, 1, 2, 0, 1, 2, 3, 0, 1, 2, 3, 2, 3, 3)
GROUP_PAIR = (0, 0, 1, 1, 0, 2, 2, 1, 0, 3, 3, 2, 1, 3, 2, 3)
GROUP_SEND = (0, 1, 2, 3, 4, 5, 6, 7, 0, 8, 9, 10, 0, 11, 0, 0)
SENDS = 12
BLOCKS = 64


def lookup(index, values):
    out = jnp.int32(values[-1])
    for position in range(len(values) - 1):
        out = jnp.where(index == position, jnp.int32(values[position]), out)
    return out


def head_kernel(hidden_t, d_logits, w_out,
                grad_t, w_own_t, grad_hidden, recv_core, recv_first, recv_second,
                dz_buf, wo_buf, acc, g_acc, add_core, add_first, add_second, stage, fin, fin_w,
                dz_sem, wo_sem, core_sem, first_sem, second_sem, stage_sem, add_sem, fin_sem, fin_w_sem):
    me = lax.axis_index(DATA_AXIS)
    core = lax.rem(me, 2)
    pos_x = lax.rem(me // 2, 2)
    pos_y = me // 4
    partner = me + 1 - 2 * core
    near_x = me + 2 - 4 * pos_x
    near_y = me + 4 - 8 * pos_y

    barrier = pltpu.get_barrier_semaphore()
    for other in (partner, near_x, near_y):
        pl.semaphore_signal(barrier, inc=1, device_id=(other,), device_id_type=MESH)
    pl.semaphore_wait(barrier, 3)

    def decode(n):
        group = n // 4
        half = lax.rem(n, 2)
        own = lax.rem(n // 2, 2)
        rel = lookup(group, GROUP_DEST)
        far_first = 1 - rel // 2
        far_second = 1 - lax.rem(rel, 2)
        sub = 2 * lookup(group, GROUP_PAIR) + half
        delta_x = jnp.where(half == 0, far_first, far_second)
        delta_y = jnp.where(half == 0, far_second, far_first)
        dest_x = pos_x + delta_x - 2 * pos_x * delta_x
        dest_y = pos_y + delta_y - 2 * pos_y * delta_y
        dest_core = jnp.where(own == 1, core, 1 - core)
        dest = (dest_y * 2 + dest_x) * 2 + dest_core
        col = pl.multiple_of(((125 * dest) // 4 + 4 * sub) * 128, 128)
        return group, half, own, rel, sub, dest, col

    def fetch(n):
        col = decode(n)[-1]
        slot = lax.rem(n, 2)
        return (pltpu.make_async_copy(d_logits.at[:, pl.ds(col, BLK)], dz_buf.at[slot], dz_sem.at[slot]),
                pltpu.make_async_copy(w_out.at[:, pl.ds(col, BLK)], wo_buf.at[slot], wo_sem.at[slot]))

    def send(slot, target_ref, recv_sem, device):
        return pltpu.make_async_remote_copy(
            src_ref=stage.at[slot], dst_ref=target_ref, send_sem=stage_sem.at[slot], recv_sem=recv_sem,
            device_id=(device,), device_id_type=MESH)

    def to_core(slot, index):
        return send(slot, recv_core.at[index], core_sem.at[index], partner)

    def to_first(slot, index, device):
        return send(slot, recv_first.at[index], first_sem.at[index], device)

    def to_second(slot, index, device):
        return send(slot, recv_second.at[index], second_sem.at[index], device)

    def wait_slot(slot):
        to_core(slot, 0).wait_send()

    for copy in fetch(jnp.int32(0)):
        copy.start()
    g_acc[...] = jnp.zeros_like(g_acc)

    def body(n, carry):
        group, half, own, rel, sub, dest, col = decode(n)
        slot = lax.rem(n, 2)

        @pl.when(n + 1 < BLOCKS)
        def _():
            for copy in fetch(n + 1):
                copy.start()

        core_index = sub * 4 + rel
        first_index = sub * 2 + 1 - lax.rem(rel, 2)
        needs_first = jnp.logical_and(own == 1, rel >= 2)
        is_final = jnp.logical_and(own == 1, rel == 3)
        load_core = pltpu.make_async_copy(recv_core.at[core_index], add_core, add_sem.at[0])
        load_first = pltpu.make_async_copy(recv_first.at[first_index], add_first, add_sem.at[1])
        load_second = pltpu.make_async_copy(recv_second.at[sub], add_second, add_sem.at[2])

        for copy in fetch(n):
            copy.wait()

        @pl.loop(0, BLK // 256)
        def _(tile):
            cols = pl.ds(pl.multiple_of(tile * 256, 256), 256)
            acc[:, cols] = jnp.dot(hidden_t[...], dz_buf[slot, :, cols], preferred_element_type=jnp.float32)

        @pl.when(own == 1)
        def _():
            to_core(0, core_index).wait_recv()
            load_core.start()

        @pl.when(needs_first)
        def _():
            to_first(0, first_index, near_x).wait_recv()
            load_first.start()

        @pl.when(is_final)
        def _():
            to_second(0, sub, near_x).wait_recv()
            load_second.start()

        lane = lax.broadcasted_iota(jnp.int32, (1, BLK), 1) + (col - SHARD * dest)
        keep = jnp.where(jnp.logical_and(lane >= 0, lane < SHARD), 1.0, 0.0).astype(jnp.bfloat16)
        weights = wo_buf[slot] * keep

        @pl.loop(0, 4)
        def _(tile):
            rows = pl.ds(pl.multiple_of(tile * 512, 512), 512)
            g_acc[rows, :] += lax.dot_general(dz_buf[slot, rows, :], weights, (((1,), (1,)), ((), ())),
                                              preferred_element_type=jnp.float32)

        @pl.when(own == 0)
        def _():
            place = 2 * RING + lax.rem(group, 2) * 2 + half

            @pl.when(group >= 2)
            def _():
                wait_slot(place)

            stage[place] = acc[...]
            to_core(place, core_index).start()

        turn = lookup(group, GROUP_SEND)
        along_y = jnp.where(rel < 2, half, 1 - half)
        place = along_y * RING + lax.rem(turn, RING)
        device = jnp.where(along_y == 1, near_y, near_x)

        @pl.when(jnp.logical_and(own == 1, rel < 2))
        def _():
            load_core.wait()

            @pl.when(turn >= RING)
            def _():
                wait_slot(place)

            stage[place] = acc[...] + add_core[...]
            to_first(place, first_index, device).start()

        @pl.when(jnp.logical_and(own == 1, rel == 2))
        def _():
            load_core.wait()
            load_first.wait()

            @pl.when(turn >= RING)
            def _():
                wait_slot(place)

            stage[place] = acc[...] + add_core[...] + add_first[...]
            to_second(place, sub, device).start()

        @pl.when(is_final)
        def _():
            load_core.wait()
            load_first.wait()
            load_second.wait()
            rows = pl.ds(pl.multiple_of(sub * BLK, BLK), BLK)
            out_grad = pltpu.make_async_copy(fin.at[half], grad_t.at[rows], fin_sem.at[half])
            out_w = pltpu.make_async_copy(fin_w.at[half], w_own_t.at[rows], fin_w_sem.at[half])

            @pl.when(sub >= 2)
            def _():
                out_grad.wait()
                out_w.wait()

            total = acc[...] + add_core[...] + add_first[...] + add_second[...]
            fin[half] = total.T
            fin_w[half] = wo_buf[slot].T
            out_grad.start()
            out_w.start()

        return carry

    lax.fori_loop(0, BLOCKS, body, 0)

    @pl.loop(0, 4)
    def _(tile):
        rows = pl.ds(pl.multiple_of(tile * 512, 512), 512)
        grad_hidden[rows, :] = g_acc[rows, :].astype(jnp.bfloat16)

    for half in range(2):
        rows = pl.ds((SUBS - 2 + half) * BLK, BLK)
        pltpu.make_async_copy(fin.at[half], grad_t.at[rows], fin_sem.at[half]).wait()
        pltpu.make_async_copy(fin_w.at[half], w_own_t.at[rows], fin_w_sem.at[half]).wait()
    for place in range(2 * RING + DRING):
        wait_slot(place)


def head_gradient(hidden, d_logits, w_out):
    tokens, dim = hidden.shape
    f32 = jnp.float32
    bf16 = jnp.bfloat16
    any_spec = pl.BlockSpec(memory_space=pl.ANY)
    vmem = pl.BlockSpec(memory_space=pltpu.VMEM)
    outs = pl.pallas_call(
        head_kernel,
        out_shape=(
            jax.ShapeDtypeStruct((SUBS * BLK, dim), f32),
            jax.ShapeDtypeStruct((SUBS * BLK, dim), bf16),
            jax.ShapeDtypeStruct((tokens, dim), bf16),
            jax.ShapeDtypeStruct((4 * SUBS, dim, BLK), f32),
            jax.ShapeDtypeStruct((2 * SUBS, dim, BLK), f32),
            jax.ShapeDtypeStruct((SUBS, dim, BLK), f32),
        ),
        in_specs=[vmem, any_spec, any_spec],
        out_specs=(any_spec, any_spec, vmem, any_spec, any_spec, any_spec),
        scratch_shapes=[
            pltpu.VMEM((2, tokens, BLK), bf16),
            pltpu.VMEM((2, dim, BLK), bf16),
            pltpu.VMEM((dim, BLK), f32),
            pltpu.VMEM((tokens, dim), f32),
            pltpu.VMEM((dim, BLK), f32),
            pltpu.VMEM((dim, BLK), f32),
            pltpu.VMEM((dim, BLK), f32),
            pltpu.VMEM((2 * RING + DRING, dim, BLK), f32),
            pltpu.VMEM((2, BLK, dim), f32),
            pltpu.VMEM((2, BLK, dim), bf16),
            pltpu.SemaphoreType.DMA((2,)),
            pltpu.SemaphoreType.DMA((2,)),
            pltpu.SemaphoreType.DMA((4 * SUBS,)),
            pltpu.SemaphoreType.DMA((2 * SUBS,)),
            pltpu.SemaphoreType.DMA((SUBS,)),
            pltpu.SemaphoreType.DMA((2 * RING + DRING,)),
            pltpu.SemaphoreType.DMA((3,)),
            pltpu.SemaphoreType.DMA((2,)),
            pltpu.SemaphoreType.DMA((2,)),
        ],
        compiler_params=pltpu.CompilerParams(collective_id=0, has_side_effects=True, vmem_limit_bytes=56 * 1024 * 1024),
        cost_estimate=pl.CostEstimate(flops=280_000_000_000, bytes_accessed=300_000_000, transcendentals=0),
        name='head_gradient',
    )(hidden.T, d_logits, w_out)
    return outs[0], outs[1], outs[2]


def gelu_tanh(values):
    return jax.nn.gelu(values, approximate=True)


def adam_update(gradient, moment_one, moment_two):
    moment_one = BETA1 * moment_one + (1.0 - BETA1) * gradient
    moment_two = BETA2 * moment_two + (1.0 - BETA2) * gradient * gradient
    direction = (moment_one / (1.0 - BETA1 ** STEP)) / (jnp.sqrt(moment_two / (1.0 - BETA2 ** STEP)) + EPS)
    return moment_one, moment_two, direction


def local_step(tokens, d_logits, w_up, w_down, w_out, proj_up, proj_down, mom_up, var_up, mom_down, var_down, mom_out, var_out):
    num_layers = w_up.shape[0]
    hidden = tokens
    saved_acts = []
    for layer_idx in range(num_layers):
        pre_act = jnp.dot(hidden, w_up[layer_idx], preferred_element_type=jnp.float32).astype(jnp.bfloat16)
        post_act = gelu_tanh(pre_act.astype(jnp.float32)).astype(jnp.bfloat16)
        saved_acts.append((hidden, pre_act, post_act))
        hidden = (hidden.astype(jnp.float32) + jnp.dot(post_act, w_down[layer_idx], preferred_element_type=jnp.float32)).astype(jnp.bfloat16)

    head_window, w_own_window, grad_hidden = head_gradient(hidden, d_logits, w_out)

    me = lax.axis_index(DATA_AXIS)
    offset = 32 * lax.rem(me, 4)
    head_part = lax.dynamic_slice_in_dim(head_window, offset, SHARD, axis=0)
    w_part = lax.dynamic_slice_in_dim(w_own_window, offset, SHARD, axis=0)
    m_out, v_out, dir_out = adam_update(head_part, mom_out.T, var_out.T)
    w_part = (w_part.astype(jnp.float32) - LR_HEAD * dir_out).astype(jnp.bfloat16)
    w_out_new = lax.all_gather(w_part, DATA_AXIS, axis=0, tiled=True).T

    ups = []
    downs = []
    for layer_idx in reversed(range(num_layers)):
        hidden_in, pre_act, post_act = saved_acts[layer_idx]
        grad_down = jnp.einsum('tf,td->fd', post_act, grad_hidden, preferred_element_type=jnp.float32)
        d_post = jnp.einsum('td,fd->tf', grad_hidden, w_down[layer_idx], preferred_element_type=jnp.float32)
        gelu_pull = jax.vjp(gelu_tanh, pre_act.astype(jnp.float32))[1]
        d_pre = gelu_pull(d_post)[0].astype(jnp.bfloat16)
        grad_up = jnp.einsum('tf,td->fd', d_pre, hidden_in, preferred_element_type=jnp.float32)
        if layer_idx > 0:
            grad_hidden = (grad_hidden.astype(jnp.float32) + jnp.einsum('tf,df->td', d_pre, w_up[layer_idx], preferred_element_type=jnp.float32)).astype(jnp.bfloat16)
        low_up = jnp.dot(grad_up, proj_up[layer_idx].astype(jnp.float32), preferred_element_type=jnp.float32)
        low_down = jnp.dot(grad_down, proj_down[layer_idx].astype(jnp.float32), preferred_element_type=jnp.float32)
        ups.append(low_up)
        downs.append(low_down)
    ups = ups[::-1]
    downs = downs[::-1]

    devices = lax.axis_size(DATA_AXIS)
    rank = ups[0].shape[1]
    parts = jnp.stack([low.reshape(devices, -1, rank) for low in ups + downs], axis=1)
    parts = lax.all_to_all(parts, DATA_AXIS, 0, 0, tiled=True)
    sums = jnp.sum(parts, axis=0)
    first = jnp.concatenate([jnp.swapaxes(mom_up, 1, 2), mom_down], axis=0)
    second = jnp.concatenate([jnp.swapaxes(var_up, 1, 2), var_down], axis=0)
    m_low, v_low, dir_low = adam_update(sums, first, second)
    dir_low = dir_low.astype(jnp.bfloat16)

    dir_up = lax.all_gather(dir_low[:num_layers], DATA_AXIS, axis=1, tiled=True)
    dir_down = lax.all_gather(dir_low[num_layers:], DATA_AXIS, axis=1, tiled=True)
    step_up = jnp.einsum('ldr,lfr->ldf', proj_up, dir_up, preferred_element_type=jnp.float32)
    step_down = jnp.einsum('lfr,ldr->lfd', dir_down, proj_down, preferred_element_type=jnp.float32)
    w_up_new = (w_up.astype(jnp.float32) - LR * ALPHA * step_up).astype(jnp.bfloat16)
    w_down_new = (w_down.astype(jnp.float32) - LR * ALPHA * step_down).astype(jnp.bfloat16)

    return (w_up_new, w_down_new, w_out_new,
            jnp.swapaxes(m_low[:num_layers], 1, 2), jnp.swapaxes(v_low[:num_layers], 1, 2),
            m_low[num_layers:], v_low[num_layers:],
            m_out.T, v_out.T)


def solution(mesh):
    row_spec = P(DATA_AXIS, None)
    whole = P()
    up_spec = P(None, None, DATA_AXIS)
    down_spec = P(None, DATA_AXIS, None)
    head_spec = P(None, DATA_AXIS)
    in_specs = (row_spec, row_spec, whole, whole, whole, whole, whole, up_spec, up_spec, down_spec, down_spec, head_spec, head_spec)
    out_specs = (whole, whole, whole, up_spec, up_spec, down_spec, down_spec, head_spec, head_spec)
    return jax.shard_map(local_step, mesh=mesh, in_specs=in_specs, out_specs=out_specs, check_vma=False)
```

time: 882 us -> 601 us (0.68)
  waiting for transfers between devices: 357 us -> 6.88 us
  Pallas kernels: 0 us -> 302 us
  matrix products: 244 us -> 85.8 us
  blocking collectives: 137 us -> 102 us
  local copies, waits for them, and re-layouts: 82.6 us -> 59.3 us
    reduce_scatter x1 -> x0, waiting for transfers between devices: 357 us -> none  [local_step(): lax.psum_scatter(grad_head, DATA_AXIS, scatter_dimension=1, tiled=True)]
    pallas_call x0 -> x1, Pallas kernels: none -> 302 us  [head_gradient(): pl.pallas_call(head_kernel, out_shape=(jax.ShapeDtypeStruct((SUBS * BLK,...]
    dot_general x17 -> x16, matrix products: 244 us -> 85.8 us  [the longest x2 22.9 us: local_step(): jnp.einsum('tf,td->fd', d_pre, hidden_in, preferred_element_type=jnp.floa...]
    unnamed x4 -> x0, blocking collectives: 88.4 us -> none
    all_to_all x0 -> x1, blocking collectives: none -> 66.2 us  [local_step(): parts = lax.all_to_all(parts, DATA_AXIS, 0, 0, tiled=True)]
    unnamed x42 -> x34, local copies, waits for them, and re-layouts: 68.5 us -> 48.3 us
    transpose x0 -> x1, other arithmetic: none -> 17.9 us  [local_step(): return (w_up_new, w_down_new, w_out_new, jnp.swapaxes(m_low[:num_layers],...]
    convert_element_type x1, other arithmetic: 18.8 us -> 2.04 us  [local_step(): dir_low = dir_low.astype(jnp.bfloat16)]
  transfers between devices with their start and end apart: 6 -> 1, of which waited for: 1 -> 1; matrix products, arithmetic and copies ran while one was open for 32% -> 13% of each run, Pallas kernels for 0% -> 0%
where the time goes in v1:
time: 601 us; the launch traced here: 591 us
  Pallas kernels  302 us (50%)
  blocking collectives  102 us (17%)
  matrix products  85.8 us (14%)
  local copies, waits for them, and re-layouts  59.3 us (10%)
  other arithmetic  20.7 us (3%)
  between operations  14.8 us (2%)
  waiting for transfers between devices  6.88 us (1%)
    pallas_call x1, Pallas kernels, head_gradient(): pl.pallas_call(head_kernel, out_shape=(jax.ShapeDtypeStruct((SUBS * BLK,...  302 us
    all_to_all x1, blocking collectives, local_step(): parts = lax.all_to_all(parts, DATA_AXIS, 0, 0, tiled=True)  66.2 us
    unnamed x34, local copies, waits for them, and re-layouts  48.3 us
    dot_general x2, matrix products, local_step(): jnp.einsum('tf,td->fd', d_pre, hidden_in, preferred_element_type=jnp.floa...  22.9 us
    all_gather x1, blocking collectives, local_step(): lax.all_gather(dir_low[num_layers:], DATA_AXIS, axis=1, tiled=True)  18 us
    transpose x1, other arithmetic, local_step(): return (w_up_new, w_down_new, w_out_new, jnp.swapaxes(m_low[:num_layers],...  17.9 us
    all_gather x1, blocking collectives, local_step(): dir_up = lax.all_gather(dir_low[:num_layers], DATA_AXIS, axis=1, tiled=True)  17.6 us
    dot_general x2, matrix products, local_step(): jnp.einsum('tf,td->fd', post_act, grad_hidden, preferred_element_type=jnp...  17.3 us
  transfers between devices with their start and end apart: 1, of which 1 were waited for; matrix products, arithmetic and copies ran while one was open for 13% of the time, Pallas kernels for 0%

profile of v1, /device:TPU:0, one launch (start us, length us, event | category | flops | bytes accessed | tf_op | source)
XLA Modules:
  0.0 591.5 jit_solution(8415203949382121102)
XLA Ops:
  7.2 0.0 all-gather.2.cloned.1.call-start
  7.2 2.9 copy.46
  10.2 0.0 copy-start.5
  10.2 5.3 convolution_convert_fusion.1
  15.4 0.0 copy-done.5
  15.5 0.0 copy-start.11
  15.5 0.0 copy-start.2
  15.5 5.3 add_convert_fusion.2
  20.8 0.0 copy-done.11
  20.8 0.0 copy-done.2
  20.8 0.0 copy-start.13
  20.8 3.3 convolution_convert_fusion
  24.1 0.0 copy-done.13
  24.1 0.0 copy-start.12
  24.2 2.5 copy-done.12
  26.6 6.3 %fusion.29.hidden_t = bf16[512,2048]{1,0:T(8,128)(2,1)} fusion(bf16[2048,512]{0,1:T(8,128)(2,1)S(1)} %add_convert_fusion.2, bf16[2,1376,512]{2,1,0:T(8,128)(2,1)S(1)} %copy-done.5, bf16[2048,1376]{0,1:T(8,128)(2,1)S(1)} %convolution_convert_fusion), kind=kOutput, calls=%fused_computation.50 | convolution fusion | flops 2917007360 | bytes 11239424 | tf_op jit(solution)/shard_map/dot_general | solution.py:292
  32.9 0.0 copy-start
  32.9 302.1 %head_gradient.1 = (f32[4096,512]{1,0:T(8,128)}, bf16[4096,512]{1,0:T(8,128)(2,1)}, bf16[2048,512]{1,0:T(8,128)(2,1)}, f32[32,512,512]{2,1,0:T(8,128)}, f32[16,512,512]{2,1,0:T(8,128)}, /*index=5*/f32[8,512,512]{2,1,0:T(8,128)}) custom-call(bf16[512,2048]{1,0:T(8,128)(2,1)} %fusion.29.hidden_t, bf16[2048,32000]{1,0:T(8,128)(2,1)} %d_logits.1, ...), custom_call_target="tpu_custom_call" | custom-call | flops 280000004096 | bytes 300000000 | tf_op jit(solution)/shard_map/head_gradient/pallas_call | solution.py:233
  335.1 0.0 copy-done
  335.1 17.9 %fusion.31 = (f32[512,4000]{0,1:T(8,128)}, bf16[4000,512]{1,0:T(8,128)(2,1)}, f32[512,4000]{0,1:T(8,128)}) fusion(f32[4096,512]{1,0:T(8,128)} %get-tuple-element.14, s32[]{:T(128)S(6)} %select_n.4, f32[512,4000]{0,1:T(8,128)S(1)} %copy-done, f32[512,4000]{0,1:T(8,128)} %param.24, bf16[4096,512]{1,0:T(8,128)(2,1)} %get-tuple-element.13), kind=kLoop, calls=%fused_computation.52 | loop fusion | flops 30720000 | bytes 49152004 | tf_op jit(solution)/shard_map/transpose | solution.py:342
  352.9 0.0 all-gather.2.cloned.1.call-update
  353.0 0.0 copy-start.3
  353.0 0.0 copy-start.15
  353.0 12.0 %fusion.4 = bf16[2048,1376]{0,1:T(8,128)(2,1)S(1)} fusion(bf16[2048,1376]{0,1:T(8,128)(2,1)} %copy-done.12, bf16[2048,512]{1,0:T(8,128)(2,1)} %get-tuple-element.12, bf16[2,1376,512]{2,1,0:T(8,128)(2,1)} %param.16), kind=kOutput, calls=%fused_computation.15 | convolution fusion | flops 2944860160 | bytes 14778368 | tf_op jit(solution)/shard_map/td,fd->tf/dot_general | solution.py:309
  365.0 0.0 copy-start.14
  365.0 2.5 copy-done.14
  367.5 0.0 copy-done.3
  367.5 0.0 copy-done.15
  367.5 5.1 add_convert_fusion
  372.6 0.0 copy-done.6
  372.6 15.4 %fusion.20 = bf16[1376,512]{1,0:T(8,128)(2,1)} fusion(bf16[2048,512]{1,0:T(8,128)(2,1)} %param.13, bf16[2048,1376]{0,1:T(8,128)(2,1)} %copy-done.11, bf16[2048,512]{1,0:T(8,128)(2,1)} %add_convert_fusion, bf16[2,1376,512]{2,1,0:T(8,128)(2,1)S(1)} %copy-done.6), kind=kOutput, calls=%fused_computation.31 | convolution fusion | flops 5830541312 | bytes 12648448 | tf_op jit(solution)/shard_map/tf,td->fd/dot_general | solution.py:312
  388.0 1.7 reshape.42
  389.7 8.6 %fusion.70 = bf16[1376,512]{1,0:T(8,128)(2,1)} fusion(bf16[2048,512]{1,0:T(8,128)(2,1)} %add_convert_fusion, bf16[2048,1376]{0,1:T(8,128)(2,1)} %copy-done.11), kind=kOutput, calls=%fused_computation.97 | convolution fusion | flops 2913861632 | bytes 9142272 | tf_op jit(solution)/shard_map/tf,td->fd/dot_general | solution.py:308
  398.3 1.5 reshape.44
  399.8 7.5 %fusion.78 = bf16[1376,512]{1,0:T(8,128)(2,1)} fusion(bf16[2048,1376]{0,1:T(8,128)(2,1)} %copy-done.14, bf16[2048,512]{0,1:T(8,128)(2,1)} %copy-done.13), kind=kOutput, calls=%fused_computation.101 | convolution fusion | flops 2885681152 | bytes 9142272 | tf_op jit(solution)/shard_map/tf,td->fd/dot_general | solution.py:312
  407.3 2.3 reshape.43
  409.6 8.7 %fusion.67 = bf16[1376,512]{1,0:T(8,128)(2,1)} fusion(bf16[2048,512]{1,0:T(8,128)(2,1)} %get-tuple-element.12, bf16[2048,1376]{0,1:T(8,128)(2,1)} %copy-done.12), kind=kOutput, calls=%fused_computation.96 | convolution fusion | flops 2913861632 | bytes 9142272 | tf_op jit(solution)/shard_map/tf,td->fd/dot_general | solution.py:308
  418.3 2.6 reshape.45
  420.8 0.0 copy-done.8
  420.8 0.5 convolution_bitcast_fusion.3
  421.4 1.9 convolution_bitcast_fusion.2
  423.3 0.0 copy-done.9
  423.3 0.5 convolution_bitcast_fusion.1
  423.8 0.0 copy-done.1
  423.8 0.5 convolution_bitcast_fusion
  424.4 0.2 pad_maximum_fusion
  424.6 1.8 copy.49
  426.4 66.2 %all_to_all.5 = f32[8,4,172,128]{3,1,2,0:T(4,128)S(1)} all-to-all(f32[8,4,172,128]{3,1,2,0:T(4,128)S(1)} %copy.49), channel_id=1, replica_groups=mesh['data'=8] {'data'}, dimensions={0} | all-to-all | bytes 5636096 | tf_op jit(solution)/shard_map/all_to_all | solution.py:325
  492.6 0.6 reduce_sum.9
  493.2 0.0 copy-start.4
  493.2 0.0 copy-start.7
  493.2 0.0 copy-start.10
  493.2 2.0 fusion.52
  495.2 0.1 fusion.77
  495.4 17.6 %all_gather.9 = bf16[2,1376,128]{2,0,1:T(2,128)(2,1)S(1)} all-gather(bf16[2,172,128]{2,0,1:T(2,128)(2,1)S(1)} %get-tuple-element.53), channel_id=1, replica_groups=mesh['data'=8] {'data'}, dimensions={1}, use_global_device_ids=true | all-gather | bytes 792576 | tf_op jit(solution)/shard_map/all_gather | solution.py:332
  513.0 18.0 %all_gather.10 = bf16[2,1376,128]{2,0,1:T(2,128)(2,1)S(1)} all-gather(bf16[2,172,128]{2,0,1:T(2,128)(2,1)S(1)} %get-tuple-element.52), channel_id=1, replica_groups=mesh['data'=8] {'data'}, dimensions={1}, use_global_device_ids=true | all-gather | bytes 792576 | tf_op jit(solution)/shard_map/all_gather | solution.py:333
  531.0 1.1 fusion.75
  532.1 0.0 copy-done.4
  532.1 2.5 fusion.22
  534.6 0.0 copy-done.7
  534.6 0.0 copy-done.10
  534.6 2.5 subtract_convert_fusion.1
  537.0 6.9 %all-gather.2.cloned.1.call-done = bf16[32000,512]{1,0:T(8,128)(2,1)} async-done(((bf16[4000,512]{1,0:T(8,128)(2,1)}), bf16[32000,512]{1,0:T(8,128)(2,1)}) %all-gather.2.cloned.1.call-update) | async-done | bytes 32768016 | tf_op jit(solution)/shard_map/all_gather | solution.py:302
  543.9 40.3 %copy.52 = bf16[512,32000]{1,0:T(8,128)(2,1)} copy(bf16[512,32000]{0,1:T(8,128)(2,1)} %bitcast.88) | data formatting | bytes 65536000
  (4 shorter events, 0.0 us)
Async XLA Ops:
  7.2 536.7 %all-gather.2.cloned.1.call-start = ((), (), s32[]{:S(2)}) async-start(), calls=%async_computation.1 | async-start | bytes 36864000 | tf_op jit(solution)/shard_map/all_gather | solution.py:302
  10.2 5.3 copy-start.5
  15.5 5.4 copy-start.11
  15.5 5.4 copy-start.2
  20.8 3.3 copy-start.13
  24.1 2.5 copy-start.12
  32.9 302.2 %copy-start = (f32[512,4000]{0,1:T(8,128)S(1)}, f32[512,4000]{0,1:T(8,128)}, u32[]{:S(2)}) copy-start(f32[512,4000]{0,1:T(8,128)} %param.25) | copy-start | bytes 24576004
  353.0 14.5 %copy-start.3 = (bf16[2,512,1376]{1,2,0:T(8,128)(2,1)S(1)}, bf16[2,512,1376]{1,2,0:T(8,128)(2,1)}, u32[]{:S(2)}) copy-start(bf16[2,512,1376]{1,2,0:T(8,128)(2,1)} %param.15) | copy-start | bytes 8454148
  353.0 14.5 %copy-start.15 = (bf16[2048,512]{1,0:T(8,128)(2,1)S(1)}, bf16[2048,512]{1,0:T(8,128)(2,1)}, u32[]{:S(2)}) copy-start(bf16[2048,512]{1,0:T(8,128)(2,1)} %get-tuple-element.12) | copy-start | bytes 6291460
  365.0 2.5 copy-start.14
  367.5 5.1 copy-start.6
  409.6 11.2 %copy-start.8 = (bf16[2,512,128]{2,1,0:T(8,128)(2,1)S(1)}, bf16[2,512,128]{2,1,0:T(8,128)(2,1)}, u32[]{:S(2)}) copy-start(bf16[2,512,128]{2,1,0:T(8,128)(2,1)} %param.18) | copy-start | bytes 786436
  418.3 5.0 copy-start.9
  420.8 3.0 copy-start.1
  493.2 39.0 %copy-start.4 = (bf16[2,512,1376]{1,2,0:T(8,128)(2,1)S(1)}, bf16[2,512,1376]{1,2,0:T(8,128)(2,1)}, u32[]{:S(2)}) copy-start(bf16[2,512,1376]{1,2,0:T(8,128)(2,1)} %param.15) | copy-start | bytes 8454148
  493.2 41.4 %copy-start.7 = (bf16[2,1376,512]{2,1,0:T(8,128)(2,1)S(1)}, bf16[2,1376,512]{2,1,0:T(8,128)(2,1)}, u32[]{:S(2)}) copy-start(bf16[2,1376,512]{2,1,0:T(8,128)(2,1)} %param.16) | copy-start | bytes 8454148
  493.2 41.4 %copy-start.10 = (bf16[2,512,128]{2,1,0:T(8,128)(2,1)S(1)}, bf16[2,512,128]{2,1,0:T(8,128)(2,1)}, u32[]{:S(2)}) copy-start(bf16[2,512,128]{2,1,0:T(8,128)(2,1)} %param.19) | copy-start | bytes 786436
Sparse Core Ops, SparseCore 0:
  353.1 190.7 all-gather.1

commit v2 on v1

--- a/solution.py
+++ b/solution.py
@@ -21,6 +21,7 @@
 SUBS = 8
 SHARD = 4000
 RING = 6
+EDGE = 96
 DRING = 4
 
 GROUP_DEST = (0, 1, 0, 1, 2, 0, 1, 2, 3, 0, 1, 2, 3, 2, 3, 3)
@@ -37,10 +38,21 @@
     return out
 
 
-def head_kernel(hidden_t, d_logits, w_out,
-                grad_t, w_own_t, grad_hidden, recv_core, recv_first, recv_second,
-                dz_buf, wo_buf, acc, g_acc, add_core, add_first, add_second, stage, fin, fin_w,
-                dz_sem, wo_sem, core_sem, first_sem, second_sem, stage_sem, add_sem, fin_sem, fin_w_sem):
+def gelu_tanh(values):
+    return jax.nn.gelu(values, approximate=True)
+
+
+def adam_update(gradient, moment_one, moment_two):
+    moment_one = BETA1 * moment_one + (1.0 - BETA1) * gradient
+    moment_two = BETA2 * moment_two + (1.0 - BETA2) * gradient * gradient
+    direction = (moment_one / (1.0 - BETA1 ** STEP)) / (jnp.sqrt(moment_two / (1.0 - BETA2 ** STEP)) + EPS)
+    return moment_one, moment_two, direction
+
+
+def head_kernel(hidden_t, d_logits, w_out, mom, var, edge,
+                w_new, mom_new, var_new, grad_hidden, recv_core, recv_first, recv_second,
+                dz_buf, wo_buf, acc, g_acc, add_core, add_first, add_second, stage, moments, fin_w,
+                dz_sem, wo_sem, core_sem, first_sem, second_sem, stage_sem, add_sem, load_sem, edge_sem, store_sem, fin_sem):
     me = lax.axis_index(DATA_AXIS)
     core = lax.rem(me, 2)
     pos_x = lax.rem(me // 2, 2)
@@ -94,6 +106,46 @@
     def wait_slot(slot):
         to_core(slot, 0).wait_send()
 
+    shift = 32 * lax.rem(me, 4)
+
+    def moment_loads(sub, half):
+        first_row = jnp.clip(BLK * sub - shift, 0, SHARD - BLK)
+        place = pl.multiple_of(EDGE + first_row + shift - BLK * sub, 32)
+        rows = pl.ds(pl.multiple_of(first_row, 32), BLK)
+        return [pltpu.make_async_copy(source.at[rows], moments.at[half, kind, pl.ds(place, BLK)], load_sem.at[half, kind])
+                for kind, source in enumerate((mom, var))]
+
+    def edge_loads(half):
+        place = pl.ds(pl.multiple_of(BLK + shift, 32), EDGE)
+        return [pltpu.make_async_copy(edge.at[kind], moments.at[half, kind, place], edge_sem.at[half, kind])
+                for kind in range(2)]
+
+    def moment_stores(sub, half):
+        pieces = [(None, EDGE, BLK - 2 * EDGE)]
+        for step in range(3):
+            pieces.append((jnp.logical_or(sub > 0, 32 * step >= shift), 32 * step, 32))
+            pieces.append((jnp.logical_or(sub < SUBS - 1, 32 * step < shift), BLK - EDGE + 32 * step, 32))
+        out = []
+        for position, (needed, row, size) in enumerate(pieces):
+            target = jnp.maximum(BLK * sub - shift + row, 0)
+            rows = pl.ds(pl.multiple_of(target, 32), size)
+            for kind, result in enumerate((mom_new, var_new)):
+                out.append((needed, pltpu.make_async_copy(
+                    moments.at[half, kind, pl.ds(EDGE + row, size)], result.at[rows], store_sem.at[half, kind, position])))
+        return out
+
+    def weight_store(sub, half):
+        cols = pl.ds(pl.multiple_of(sub * BLK, BLK), BLK)
+        return pltpu.make_async_copy(fin_w.at[half], w_new.at[:, cols], fin_sem.at[half])
+
+    def for_stores(sub, half, action):
+        for needed, copy in moment_stores(sub, half):
+            if needed is None:
+                action(copy)
+            else:
+                pl.when(needed)(functools.partial(action, copy))
+        action(weight_store(sub, half))
+
     for copy in fetch(jnp.int32(0)):
         copy.start()
     g_acc[...] = jnp.zeros_like(g_acc)
@@ -135,8 +187,84 @@
 
         @pl.when(is_final)
         def _():
+            @pl.when(sub >= 2)
+            def _():
+                for_stores(sub - 2, half, lambda copy: copy.wait())
+
+            for copy in moment_loads(sub, half):
+                copy.start()
+
+            @pl.when(sub == SUBS - 1)
+            def _():
+                for copy in edge_loads(half):
+                    copy.start()
+
             to_second(0, sub, near_x).wait_recv()
             load_second.start()
+
+        @pl.when(own == 0)
+        def _():
+            place = 2 * RING + lax.rem(group, 2) * 2 + half
+
+            @pl.when(group >= 2)
+            def _():
+                wait_slot(place)
+
+            stage[place] = acc[...]
+            to_core(place, core_index).start()
+
+        turn = lookup(group, GROUP_SEND)
+        along_y = jnp.where(rel < 2, half, 1 - half)
+        place = along_y * RING + lax.rem(turn, RING)
+        device = jnp.where(along_y == 1, near_y, near_x)
+
+        @pl.when(jnp.logical_and(own == 1, rel < 2))
+        def _():
+            load_core.wait()
+
+            @pl.when(turn >= RING)
+            def _():
+                wait_slot(place)
+
+            stage[place] = acc[...] + add_core[...]
+            to_first(place, first_index, device).start()
+
+        @pl.when(jnp.logical_and(own == 1, rel == 2))
+        def _():
+            load_core.wait()
+            load_first.wait()
+
+            @pl.when(turn >= RING)
+            def _():
+                wait_slot(place)
+
+            stage[place] = acc[...] + add_core[...] + add_first[...]
+            to_second(place, sub, device).start()
+
+        @pl.when(is_final)
+        def _():
+            load_core.wait()
+            load_first.wait()
+            load_second.wait()
+            for copy in moment_loads(sub, half):
+                copy.wait()
+
+            @pl.when(sub == SUBS - 1)
+            def _():
+                for copy in edge_loads(half):
+                    copy.wait()
+
+            @pl.loop(0, BLK // 128)
+            def _(tile):
+                cols = pl.ds(pl.multiple_of(tile * 128, 128), 128)
+                rows = pl.ds(pl.multiple_of(EDGE + tile * 128, 32), 128)
+                total = acc[:, cols] + add_core[:, cols] + add_first[:, cols] + add_second[:, cols]
+                first, second, direction = adam_update(total.T, moments[half, 0, rows, :], moments[half, 1, rows, :])
+                moments[half, 0, rows, :] = first
+                moments[half, 1, rows, :] = second
+                fin_w[half, :, cols] = (wo_buf[slot, :, cols].astype(jnp.float32) - LR_HEAD * direction.T).astype(jnp.bfloat16)
+
+            for_stores(sub, half, lambda copy: copy.start())
 
         lane = lax.broadcasted_iota(jnp.int32, (1, BLK), 1) + (col - SHARD * dest)
         keep = jnp.where(jnp.logical_and(lane >= 0, lane < SHARD), 1.0, 0.0).astype(jnp.bfloat16)
@@ -148,65 +276,6 @@
             g_acc[rows, :] += lax.dot_general(dz_buf[slot, rows, :], weights, (((1,), (1,)), ((), ())),
                                               preferred_element_type=jnp.float32)
 
-        @pl.when(own == 0)
-        def _():
-            place = 2 * RING + lax.rem(group, 2) * 2 + half
-
-            @pl.when(group >= 2)
-            def _():
-                wait_slot(place)
-
-            stage[place] = acc[...]
-            to_core(place, core_index).start()
-
-        turn = lookup(group, GROUP_SEND)
-        along_y = jnp.where(rel < 2, half, 1 - half)
-        place = along_y * RING + lax.rem(turn, RING)
-        device = jnp.where(along_y == 1, near_y, near_x)
-
-        @pl.when(jnp.logical_and(own == 1, rel < 2))
-        def _():
-            load_core.wait()
-
-            @pl.when(turn >= RING)
-            def _():
-                wait_slot(place)
-
-            stage[place] = acc[...] + add_core[...]
-            to_first(place, first_index, device).start()
-
-        @pl.when(jnp.logical_and(own == 1, rel == 2))
-        def _():
-            load_core.wait()
-            load_first.wait()
-
-            @pl.when(turn >= RING)
-            def _():
-                wait_slot(place)
-
-            stage[place] = acc[...] + add_core[...] + add_first[...]
-            to_second(place, sub, device).start()
-
-        @pl.when(is_final)
-        def _():
-            load_core.wait()
-            load_first.wait()
-            load_second.wait()
-            rows = pl.ds(pl.multiple_of(sub * BLK, BLK), BLK)
-            out_grad = pltpu.make_async_copy(fin.at[half], grad_t.at[rows], fin_sem.at[half])
-            out_w = pltpu.make_async_copy(fin_w.at[half], w_own_t.at[rows], fin_w_sem.at[half])
-
-            @pl.when(sub >= 2)
-            def _():
-                out_grad.wait()
-                out_w.wait()
-
-            total = acc[...] + add_core[...] + add_first[...] + add_second[...]
-            fin[half] = total.T
-            fin_w[half] = wo_buf[slot].T
-            out_grad.start()
-            out_w.start()
-
         return carry
 
     lax.fori_loop(0, BLOCKS, body, 0)
@@ -217,14 +286,12 @@
         grad_hidden[rows, :] = g_acc[rows, :].astype(jnp.bfloat16)
 
     for half in range(2):
-        rows = pl.ds((SUBS - 2 + half) * BLK, BLK)
-        pltpu.make_async_copy(fin.at[half], grad_t.at[rows], fin_sem.at[half]).wait()
-        pltpu.make_async_copy(fin_w.at[half], w_own_t.at[rows], fin_w_sem.at[half]).wait()
+        for_stores(SUBS - 2 + half, half, lambda copy: copy.wait())
     for place in range(2 * RING + DRING):
         wait_slot(place)
 
 
-def head_gradient(hidden, d_logits, w_out):
+def head_update(hidden, d_logits, w_out, mom_t, var_t, edge):
     tokens, dim = hidden.shape
     f32 = jnp.float32
     bf16 = jnp.bfloat16
@@ -233,15 +300,16 @@
     outs = pl.pallas_call(
         head_kernel,
         out_shape=(
-            jax.ShapeDtypeStruct((SUBS * BLK, dim), f32),
-            jax.ShapeDtypeStruct((SUBS * BLK, dim), bf16),
+            jax.ShapeDtypeStruct((dim, SUBS * BLK), bf16),
+            jax.ShapeDtypeStruct(mom_t.shape, f32),
+            jax.ShapeDtypeStruct(var_t.shape, f32),
             jax.ShapeDtypeStruct((tokens, dim), bf16),
             jax.ShapeDtypeStruct((4 * SUBS, dim, BLK), f32),
             jax.ShapeDtypeStruct((2 * SUBS, dim, BLK), f32),
             jax.ShapeDtypeStruct((SUBS, dim, BLK), f32),
         ),
-        in_specs=[vmem, any_spec, any_spec],
-        out_specs=(any_spec, any_spec, vmem, any_spec, any_spec, any_spec),
+        in_specs=[vmem] + [any_spec] * 5,
+        out_specs=(any_spec, any_spec, any_spec, vmem, any_spec, any_spec, any_spec),
         scratch_shapes=[
             pltpu.VMEM((2, tokens, BLK), bf16),
             pltpu.VMEM((2, dim, BLK), bf16),
@@ -251,8 +319,8 @@
             pltpu.VMEM((dim, BLK), f32),
             pltpu.VMEM((dim, BLK), f32),
             pltpu.VMEM((2 * RING + DRING, dim, BLK), f32),
-            pltpu.VMEM((2, BLK, dim), f32),
-            pltpu.VMEM((2, BLK, dim), bf16),
+            pltpu.VMEM((2, 2, BLK + 2 * EDGE, dim), f32),
+            pltpu.VMEM((2, dim, BLK), bf16),
             pltpu.SemaphoreType.DMA((2,)),
             pltpu.SemaphoreType.DMA((2,)),
             pltpu.SemaphoreType.DMA((4 * SUBS,)),
@@ -260,25 +328,16 @@
             pltpu.SemaphoreType.DMA((SUBS,)),
             pltpu.SemaphoreType.DMA((2 * RING + DRING,)),
             pltpu.SemaphoreType.DMA((3,)),
-            pltpu.SemaphoreType.DMA((2,)),
+            pltpu.SemaphoreType.DMA((2, 2)),
+            pltpu.SemaphoreType.DMA((2, 2)),
+            pltpu.SemaphoreType.DMA((2, 2, 7)),
             pltpu.SemaphoreType.DMA((2,)),
         ],
         compiler_params=pltpu.CompilerParams(collective_id=0, has_side_effects=True, vmem_limit_bytes=56 * 1024 * 1024),
         cost_estimate=pl.CostEstimate(flops=280_000_000_000, bytes_accessed=300_000_000, transcendentals=0),
-        name='head_gradient',
-    )(hidden.T, d_logits, w_out)
-    return outs[0], outs[1], outs[2]
-
-
-def gelu_tanh(values):
-    return jax.nn.gelu(values, approximate=True)
-
-
-def adam_update(gradient, moment_one, moment_two):
-    moment_one = BETA1 * moment_one + (1.0 - BETA1) * gradient
-    moment_two = BETA2 * moment_two + (1.0 - BETA2) * gradient * gradient
-    direction = (moment_one / (1.0 - BETA1 ** STEP)) / (jnp.sqrt(moment_two / (1.0 - BETA2 ** STEP)) + EPS)
-    return moment_one, moment_two, direction
+        name='head_update',
+    )(hidden.T, d_logits, w_out, mom_t, var_t, edge)
+    return outs[:4]
 
 
 def local_step(tokens, d_logits, w_up, w_down, w_out, proj_up, proj_down, mom_up, var_up, mom_down, var_down, mom_out, var_out):
@@ -291,15 +350,12 @@
         saved_acts.append((hidden, pre_act, post_act))
         hidden = (hidden.astype(jnp.float32) + jnp.dot(post_act, w_down[layer_idx], preferred_element_type=jnp.float32)).astype(jnp.bfloat16)
 
-    head_window, w_own_window, grad_hidden = head_gradient(hidden, d_logits, w_out)
-
-    me = lax.axis_index(DATA_AXIS)
-    offset = 32 * lax.rem(me, 4)
-    head_part = lax.dynamic_slice_in_dim(head_window, offset, SHARD, axis=0)
-    w_part = lax.dynamic_slice_in_dim(w_own_window, offset, SHARD, axis=0)
-    m_out, v_out, dir_out = adam_update(head_part, mom_out.T, var_out.T)
-    w_part = (w_part.astype(jnp.float32) - LR_HEAD * dir_out).astype(jnp.bfloat16)
-    w_out_new = lax.all_gather(w_part, DATA_AXIS, axis=0, tiled=True).T
+    devices = lax.axis_size(DATA_AXIS)
+    mom_t, var_t = mom_out.T, var_out.T
+    edge = lax.ppermute(jnp.stack([mom_t[:EDGE], var_t[:EDGE]]), DATA_AXIS, [(dev, dev - 1) for dev in range(1, devices)])
+    w_window, m_out, v_out, grad_hidden = head_update(hidden, d_logits, w_out, mom_t, var_t, edge)
+    windows = lax.all_gather(w_window, DATA_AXIS, axis=0)
+    w_out_new = jnp.concatenate([windows[dev, :, (128 if dev % 4 else 0):] for dev in range(devices)], axis=1)
 
     ups = []
     downs = []
@@ -319,7 +375,6 @@
     ups = ups[::-1]
     downs = downs[::-1]
 
-    devices = lax.axis_size(DATA_AXIS)
     rank = ups[0].shape[1]
     parts = jnp.stack([low.reshape(devices, -1, rank) for low in ups + downs], axis=1)
     parts = lax.all_to_all(parts, DATA_AXIS, 0, 0, tiled=True)

time: 601 us -> 600 us (level)
  waiting for transfers between devices: 6.88 us -> 73.9 us
  blocking collectives: 102 us -> 35.9 us
  other arithmetic: 20.7 us -> 2.88 us
  Pallas kernels: 302 us -> 311 us
    all_to_all x1 -> x0, blocking collectives: 66.2 us -> none  [local_step(): parts = lax.all_to_all(parts, DATA_AXIS, 0, 0, tiled=True)]
    all_to_all x0 -> x1, waiting for transfers between devices: none -> 64.6 us  [local_step(): parts = lax.all_to_all(parts, DATA_AXIS, 0, 0, tiled=True)]
    transpose x1 -> x0, other arithmetic: 17.9 us -> none  [local_step(): return (w_up_new, w_down_new, w_out_new, jnp.swapaxes(m_low[:num_layers],...]
    pallas_call x1, Pallas kernels: 302 us -> 311 us  [head_update(): pl.pallas_call(head_kernel, out_shape=(jax.ShapeDtypeStruct((dim, SUBS *...]
    unnamed x34 -> x48, local copies, waits for them, and re-layouts: 48.3 us -> 46.5 us
  transfers between devices with their start and end apart: 1 -> 3, of which waited for: 1 -> 2; matrix products, arithmetic and copies ran while one was open for 13% -> 18% of each run, Pallas kernels for 0% -> 0%
where the time goes in v2:
time: 600 us; the launch traced here: 591 us
  Pallas kernels  311 us (52%)
  matrix products  85.1 us (14%)
  waiting for transfers between devices  73.9 us (12%)
  local copies, waits for them, and re-layouts  64.1 us (11%)
  blocking collectives  35.9 us (6%)
  between operations  14.8 us (2%)
    pallas_call x1, Pallas kernels, head_update(): pl.pallas_call(head_kernel, out_shape=(jax.ShapeDtypeStruct((dim, SUBS *...  311 us
    all_to_all x1, waiting for transfers between devices, local_step(): parts = lax.all_to_all(parts, DATA_AXIS, 0, 0, tiled=True)  64.6 us
    unnamed x48, local copies, waits for them, and re-layouts  46.5 us
    dot_general x2, matrix products, local_step(): jnp.einsum('tf,td->fd', d_pre, hidden_in, preferred_element_type=jnp.floa...  19.1 us
    all_gather x1, blocking collectives, local_step(): dir_up = lax.all_gather(dir_low[:num_layers], DATA_AXIS, axis=1, tiled=True)  18.3 us
    all_gather x1, blocking collectives, local_step(): lax.all_gather(dir_low[num_layers:], DATA_AXIS, axis=1, tiled=True)  17.6 us
    dot_general x2, matrix products, local_step(): jnp.einsum('tf,td->fd', post_act, grad_hidden, preferred_element_type=jnp...  17.2 us
  transfers between devices with their start and end apart: 3, of which 2 were waited for; matrix products, arithmetic and copies ran while one was open for 18% of the time, Pallas kernels for 0%

profile of v2, /device:TPU:0, one launch (start us, length us, event | category | flops | bytes accessed | tf_op | source)
XLA Modules:
  0.0 590.9 jit_solution(6142967547407619634)
XLA Ops:
  7.2 0.0 copy-start.1
  7.2 0.0 all-gather.3.cloned.1.call-start
  7.2 1.2 slice_bitcast_fusion.6
  8.5 1.3 collective-permute-start
  9.8 3.9 copy.44
  13.7 0.0 copy-done.1
  13.7 5.1 convolution_convert_fusion.1
  18.8 0.0 copy-start.10
  18.8 5.3 add_convert_fusion.2
  24.2 0.0 copy-start.12
  24.2 3.3 convolution_convert_fusion
  27.5 0.0 copy-start.11
  27.5 6.3 %fusion.34.hidden_t = bf16[512,2048]{1,0:T(8,128)(2,1)} fusion(bf16[2048,512]{0,1:T(8,128)(2,1)S(1)} %add_convert_fusion.2, bf16[2,1376,512]{2,1,0:T(8,128)(2,1)S(1)} %copy-done.3, bf16[2048,1376]{0,1:T(8,128)(2,1)S(1)} %convolution_convert_fusion), kind=kOutput, calls=%fused_computation.60 | convolution fusion | flops 2917007360 | bytes 11239424 | tf_op jit(solution)/shard_map/dot_general | solution.py:351
  33.8 0.0 collective-permute-done.edge
  33.8 310.6 %head_update.1 = (bf16[512,4096]{1,0:T(8,128)(2,1)}, f32[4000,512]{1,0:T(8,128)}, f32[4000,512]{1,0:T(8,128)}, bf16[2048,512]{1,0:T(8,128)(2,1)}, f32[32,512,512...) custom-call(bf16[512,2048]{1,0:T(8,128)(2,1)} %fusion.34.hidden_t, bf16[2048,32000]{1,0:T(8,128)(2,1)} %d_logits.1, ...), custom_call_target="tpu_custom_call" | custom-call | flops 280000004096 | bytes 300000000 | tf_op jit(solution)/shard_map/head_update/pallas_call | solution.py:300
  344.4 0.0 all-gather.3.cloned.1.call-update
  344.4 0.0 copy-start.13
  344.4 11.9 %fusion.4 = bf16[2048,1376]{0,1:T(8,128)(2,1)S(1)} fusion(bf16[2048,1376]{0,1:T(8,128)(2,1)} %copy-done.11, bf16[2048,512]{1,0:T(8,128)(2,1)} %get-tuple-element.13, bf16[2,1376,512]{2,1,0:T(8,128)(2,1)S(1)} %copy-done.4), kind=kOutput, calls=%fused_computation.14 | convolution fusion | flops 2944860160 | bytes 14778368 | tf_op jit(solution)/shard_map/td,fd->tf/dot_general | solution.py:365
  356.3 0.0 copy-start.14
  356.3 2.5 copy-done.14
  358.8 3.2 fusion.84
  362.0 0.3 reshape.43
  362.3 8.6 %fusion.73 = bf16[1376,512]{1,0:T(8,128)(2,1)} fusion(bf16[2048,512]{1,0:T(8,128)(2,1)} %get-tuple-element.13, bf16[2048,1376]{0,1:T(8,128)(2,1)} %copy-done.11), kind=kOutput, calls=%fused_computation.108 | convolution fusion | flops 2913861632 | bytes 9142272 | tf_op jit(solution)/shard_map/tf,td->fd/dot_general | solution.py:364
  370.9 1.6 reshape.45
  372.5 8.4 %add_convert_fusion = bf16[2048,512]{1,0:T(8,128)(2,1)} fusion(bf16[2048,512]{1,0:T(8,128)(2,1)} %get-tuple-element.13, bf16[2048,1376]{0,1:T(8,128)(2,1)} %copy-done.14, bf16[2,512,1376]{1,2,0:T(8,128)(2,1)} %param.15), kind=kOutput, calls=%fused_computation.44 | convolution fusion | flops 2888826880 | bytes 11239424 | tf_op jit(solution)/shard_map/tf,df->td/dot_general | solution.py:370
  381.0 15.9 %fusion.20 = bf16[1376,512]{1,0:T(8,128)(2,1)} fusion(bf16[2048,512]{1,0:T(8,128)(2,1)} %param.13, bf16[2048,1376]{0,1:T(8,128)(2,1)} %copy-done.10, bf16[2048,512]{1,0:T(8,128)(2,1)} %add_convert_fusion, bf16[2,1376,512]{2,1,0:T(8,128)(2,1)} %param.16), kind=kOutput, calls=%fused_computation.30 | convolution fusion | flops 5830541312 | bytes 12648448 | tf_op jit(solution)/shard_map/tf,td->fd/dot_general | solution.py:368
  396.9 2.3 reshape.42
  399.2 8.6 %fusion.76 = bf16[1376,512]{1,0:T(8,128)(2,1)} fusion(bf16[2048,512]{1,0:T(8,128)(2,1)} %add_convert_fusion, bf16[2048,1376]{0,1:T(8,128)(2,1)} %copy-done.10), kind=kOutput, calls=%fused_computation.109 | convolution fusion | flops 2913861632 | bytes 9142272 | tf_op jit(solution)/shard_map/tf,td->fd/dot_general | solution.py:364
  407.9 2.4 reshape.44
  410.2 0.0 copy-done.7
  410.2 0.5 convolution_bitcast_fusion.2
  410.8 1.9 convolution_bitcast_fusion.3
  412.7 0.0 copy-done.8
  412.7 0.5 convolution_bitcast_fusion
  413.2 0.5 convolution_bitcast_fusion.1
  413.8 0.2 pad_maximum_fusion
  414.0 3.4 copy.47
  417.4 2.4 all-to-all-start
  419.8 64.6 %all-to-all-done = f32[8,4,172,128]{3,1,2,0:T(4,128)S(1)} async-done(((f32[8,4,172,128]{3,1,2,0:T(4,128)}), f32[8,4,172,128]{3,1,2,0:T(4,128)S(1)}, u32[]{:S(2)}, u32[]{:S(2)}) %all-to-all-start) | async-done | bytes 2818080 | tf_op jit(solution)/shard_map/all_to_all | solution.py:380
  484.3 0.6 reduce_sum.9
  484.9 0.0 copy-start.2
  484.9 0.0 copy-start.5
  485.0 0.0 copy-start.9
  485.0 2.0 fusion.58
  487.0 0.1 fusion.83
  487.1 17.6 %all_gather.13 = bf16[2,1376,128]{2,0,1:T(2,128)(2,1)S(1)} all-gather(bf16[2,172,128]{2,0,1:T(2,128)(2,1)S(1)} %get-tuple-element.42), channel_id=1, replica_groups=mesh['data'=8] {'data'}, dimensions={1}, use_global_device_ids=true | all-gather | bytes 792576 | tf_op jit(solution)/shard_map/all_gather | solution.py:388
  504.8 18.3 %all_gather.12 = bf16[2,1376,128]{2,0,1:T(2,128)(2,1)S(1)} all-gather(bf16[2,172,128]{2,0,1:T(2,128)(2,1)S(1)} %get-tuple-element.43), channel_id=1, replica_groups=mesh['data'=8] {'data'}, dimensions={1}, use_global_device_ids=true | all-gather | bytes 792576 | tf_op jit(solution)/shard_map/all_gather | solution.py:387
  523.1 0.9 fusion.82
  523.9 0.9 fusion.81
  524.8 0.0 copy-done.2
  524.8 2.5 fusion.21
  527.3 2.5 subtract_convert_fusion
  529.7 9.3 %all-gather.3.cloned.1.call-done = bf16[4096,4096]{1,0:T(8,128)(2,1)} async-done(((bf16[512,4096]{1,0:T(8,128)(2,1)}), bf16[4096,4096]{1,0:T(8,128)(2,1)}) %all-gather.3.cloned.1.call-update) | async-done | bytes 33554448 | tf_op jit(solution)/shard_map/all_gather | solution.py:357
  539.0 4.7 slice_dynamic-update-slice_fusion.1
  543.7 4.4 fusion.33
  548.1 4.4 fusion.32
  552.5 4.4 fusion.31
  556.9 4.7 slice_dynamic-update-slice_fusion
  561.6 4.5 fusion.30
  566.1 4.5 fusion.29
  570.7 4.5 fusion.28
  575.2 4.2 copy.65
  579.4 0.9 slice-done.1
  580.3 3.3 copy.66
  (26 shorter events, 0.1 us)
Async XLA Ops:
  7.2 6.5 %copy-start.1 = (bf16[2,512,1376]{1,2,0:T(8,128)(2,1)S(1)}, bf16[2,512,1376]{1,2,0:T(8,128)(2,1)}, u32[]{:S(2)}) copy-start(bf16[2,512,1376]{1,2,0:T(8,128)(2,1)} %param.15) | copy-start | bytes 8454148
  7.2 531.8 %all-gather.3.cloned.1.call-start = ((), (), s32[]{:S(2)}) async-start(), calls=%async_computation.1 | async-start | bytes 37748736 | tf_op jit(solution)/shard_map/all_gather | solution.py:357
  8.5 25.3 %collective-permute-start = (f32[2,96,512]{2,1,0:T(8,128)S(1)}, f32[2,96,512]{2,1,0:T(8,128)}, u32[]{:S(2)}, u32[]{:S(2)}) collective-permute-start(f32[2,96,512]{2,1,0:T(8,128)S(1)} %pad_maximum_fusion.1), channel_id=1, source_target_pairs={{1,0},{2,1},{3,2},{4,3},{5,4},{6,5},{7,6}} | collective-permute-start | bytes 1179656 | tf_op jit(solution)/shard_map/ppermute | solution.py:355
  13.7 5.1 copy-start.3
  13.7 5.1 copy-start.6
  18.8 5.4 copy-start.10
  24.2 3.3 copy-start.12
  27.5 6.3 %copy-start.11 = (bf16[2048,1376]{0,1:T(8,128)(2,1)}, bf16[2048,1376]{0,1:T(8,128)(2,1)S(1)}, u32[]{:S(2)}) copy-start(bf16[2048,1376]{0,1:T(8,128)(2,1)S(1)} %convolution_convert_fusion) | copy-start | bytes 16908292
  33.8 310.6 %copy-start.4 = (bf16[2,1376,512]{2,1,0:T(8,128)(2,1)S(1)}, bf16[2,1376,512]{2,1,0:T(8,128)(2,1)}, u32[]{:S(2)}) copy-start(bf16[2,1376,512]{2,1,0:T(8,128)(2,1)} %param.16) | copy-start | bytes 8454148
  344.4 14.4 %copy-start.13 = (bf16[2048,512]{0,1:T(8,128)(2,1)S(1)}, bf16[2048,512]{0,1:T(8,128)(2,1)}, u32[]{:S(2)}) copy-start(bf16[2048,512]{0,1:T(8,128)(2,1)} %copy-done.12) | copy-start | bytes 6291460
  356.3 2.5 copy-start.14
  399.2 11.0 %copy-start.7 = (bf16[2,512,128]{2,1,0:T(8,128)(2,1)S(1)}, bf16[2,512,128]{2,1,0:T(8,128)(2,1)}, u32[]{:S(2)}) copy-start(bf16[2,512,128]{2,1,0:T(8,128)(2,1)} %param.18) | copy-start | bytes 786436
  407.9 4.8 copy-start.8
  410.2 3.0 copy-start
  417.4 67.0 %all-to-all-start = ((f32[8,4,172,128]{3,1,2,0:T(4,128)}), f32[8,4,172,128]{3,1,2,0:T(4,128)S(1)}, u32[]{:S(2)}, u32[]{:S(2)}) async-start(f32[8,4,172,128]{3,1,2,0:T(4,128)} %copy.47), calls=%async_computation | async-start | bytes 5636096 | tf_op jit(solution)/shard_map/all_to_all | solution.py:380
  484.9 39.9 %copy-start.2 = (bf16[2,512,1376]{1,2,0:T(8,128)(2,1)S(1)}, bf16[2,512,1376]{1,2,0:T(8,128)(2,1)}, u32[]{:S(2)}) copy-start(bf16[2,512,1376]{1,2,0:T(8,128)(2,1)} %param.15) | copy-start | bytes 8454148
  484.9 42.3 %copy-start.5 = (bf16[2,1376,512]{2,1,0:T(8,128)(2,1)S(1)}, bf16[2,1376,512]{2,1,0:T(8,128)(2,1)}, u32[]{:S(2)}) copy-start(bf16[2,1376,512]{2,1,0:T(8,128)(2,1)} %param.16) | copy-start | bytes 8454148
  485.0 42.3 %copy-start.9 = (bf16[2,512,128]{2,1,0:T(8,128)(2,1)S(1)}, bf16[2,512,128]{2,1,0:T(8,128)(2,1)}, u32[]{:S(2)}) copy-start(bf16[2,512,128]{2,1,0:T(8,128)(2,1)} %param.19) | copy-start | bytes 786436
  561.6 13.6 %slice-start.2 = ((s8[8192000]{0:T(1024)(128)(4,1)}), s8[4194304]{0:T(1024)(128)(4,1)S(1)}, s32[]{:S(2)}) async-start(s8[8192000]{0:T(1024)(128)(4,1)} %bitcast.115), calls=%async_computation.4 | async-start | bytes 8388608
  566.1 9.1 %slice-start.3 = ((s8[8192000]{0:T(1024)(128)(4,1)}), s8[3997696]{0:T(1024)(128)(4,1)S(1)}, s32[]{:S(2)}) async-start(s8[8192000]{0:T(1024)(128)(4,1)} %bitcast.115), calls=%async_computation.5 | async-start | bytes 7995392
  570.7 8.7 %slice-start = ((s8[8192000]{0:T(1024)(128)(4,1)}), s8[4194304]{0:T(1024)(128)(4,1)S(1)}, s32[]{:S(2)}) async-start(s8[8192000]{0:T(1024)(128)(4,1)} %bitcast.112), calls=%async_computation.2 | async-start | bytes 8388608
  575.2 5.1 slice-start.1
Sparse Core Ops, SparseCore 0:
  344.5 194.4 all-gather.2
